TPU v7x, 32 devices: a whole 2x2x4 slice. The times are simulated.
32 devices in a mesh: gx: 8 (over z, x), gy: 4 (over y, core).
Axes of the slice: x: 2, y: 2, z: 4, core: 2. Of those that a mesh axis runs over, the one named last changes fastest.
Arguments:
- populations: float32 [19, 48, 32, 128], P(None, 'gx', 'gy'), may hold values from 0.03 to 0.06
- cell_mass: float32 [48, 32, 128], P('gx', 'gy'), may hold values from 0.05 to 1
- cell_flags: int32 [48, 32, 128], P('gx', 'gy'), may hold values from 0 to 2
- bubble: int32 [48, 32, 128], P('gx', 'gy'), may hold values from 0 to 95, as said below
- conversion: int32 [48, 32, 128], P('gx', 'gy'), may hold values 0 or 1
- rest_volume: float32 [96], replicated, may hold values from 256 to 2048
Outputs:
- relaxed_populations: float32 [19, 48, 32, 128], P(None, 'gx', 'gy')
- new_mass: float32 [48, 32, 128], P('gx', 'gy')
- gas_density: float32 [96], replicated
Inputs may be any that keep to these rules, and one draw needn't show every extreme that they name: `cell_flags`: 0 gas, 1 interface, 2 liquid. The bubble that a gas or interface cell belongs to; unused for liquid cells. `conversion`: 1 marks an interface cell that becomes liquid in this step; unused for other cells.
All inputs are finite; a program needn't handle non-finite values. No bound on the sum of `conversion` on one device may be relied on, other than what follows from the above.
Results may differ from a plain program's by a relative error of at most 0.0003.
Values sent between devices are 32-bit elements; how exact they have to be, the bound alone decides.
No kernel may reach another device: no remote copies, remote signals or barrier semaphores. Data moves between devices by JAX's collectives and lax.ppermute only.
A program may use at most 64 MiB of HBM per device.

v0:
```python
import jax
import jax.numpy as jnp
import numpy as np
from jax import lax
from jax.sharding import PartitionSpec as P

VELOCITIES = np.array(
    [
        [0, 0, 0],
        [1, 0, 0],
        [-1, 0, 0],
        [0, 1, 0],
        [0, -1, 0],
        [0, 0, 1],
        [0, 0, -1],
        [1, 1, 0],
        [-1, -1, 0],
        [1, -1, 0],
        [-1, 1, 0],
        [1, 0, 1],
        [-1, 0, -1],
        [1, 0, -1],
        [-1, 0, 1],
        [0, 1, 1],
        [0, -1, -1],
        [0, 1, -1],
        [0, -1, 1],
    ]
)
OPPOSITE = np.array([0, 2, 1, 4, 3, 6, 5, 8, 7, 10, 9, 12, 11, 14, 13, 16, 15, 18, 17])
WEIGHTS = np.array([1.0 / 3.0] + [1.0 / 18.0] * 6 + [1.0 / 36.0] * 12)
RELAX = 1.0 / 0.6
AMBIENT = 2.0


def padded_2(cells, sides, width):
    for axis, dim in sides:
        count = lax.axis_size(axis)
        ends = count - 1
        head = lax.slice_in_dim(cells, 0, width, axis=dim)
        tail = lax.slice_in_dim(cells, cells.shape[dim] - width, cells.shape[dim], axis=dim)
        cells = jnp.concatenate(
            [
                lax.ppermute(tail, axis, [(i, (i + 1) % count) for i in range(ends)]),
                cells,
                lax.ppermute(head, axis, [((i + 1) % count, i) for i in range(ends)]),
            ],
            axis=dim,
        )
    return cells


def moments(populations):
    density = jnp.sum(populations, axis=0)
    lattice = jnp.asarray(VELOCITIES.T, jnp.float32)
    flux = jnp.einsum("kq,qxyz->kxyz", lattice, populations, precision=lax.Precision.HIGHEST)
    return (density, flux / density[None])


def unit_equilibrium(velocity):
    lattice = jnp.asarray(VELOCITIES, jnp.float32)
    project = jnp.einsum("qk,kxyz->qxyz", lattice, velocity, precision=lax.Precision.HIGHEST)
    speed = jnp.sum(velocity * velocity, axis=0)
    weights = jnp.asarray(WEIGHTS, jnp.float32)[:, None, None, None]
    return weights * (1.0 + 3.0 * project + 4.5 * project * project - 1.5 * speed[None])


def window(layer, lane, extent_rows, extent_cols):
    offset_rows, offset_cols, offset_depth = (int(value) for value in VELOCITIES[lane])
    begin_rows, begin_cols = (1 - offset_rows, 1 - offset_cols)
    return jnp.roll(
        layer[begin_rows : begin_rows + extent_rows, begin_cols : begin_cols + extent_cols],
        offset_depth,
        axis=2,
    )


def domain(inside_rows, inside_cols, lane, extent_rows, extent_cols):
    begin_rows, begin_cols = (1 - int(VELOCITIES[lane][0]), 1 - int(VELOCITIES[lane][1]))
    return (
        inside_rows[begin_rows : begin_rows + extent_rows][:, None, None]
        & inside_cols[begin_cols : begin_cols + extent_cols][None, :, None]
    )


def pull_cells(padded, inside_rows, inside_cols, populations, fraction):
    extent_rows, extent_cols = (populations.shape[1], populations.shape[2])
    pulled = [populations[0]]
    gas_side = [jnp.zeros(populations.shape[1:], jnp.bool_)]
    mass_flux = jnp.zeros(populations.shape[1:], jnp.float32)
    targets = jnp.zeros(populations.shape[1:], jnp.float32)
    for lane in range(1, 19):
        source = window(padded[lane], lane, extent_rows, extent_cols)
        source_fraction = window(padded[19], lane, extent_rows, extent_cols)
        source_status = window(padded[20], lane, extent_rows, extent_cols)
        in_domain = domain(inside_rows, inside_cols, lane, extent_rows, extent_cols)
        source_flag = jnp.where(source_status > 2.5, source_status - 3.0, source_status)
        bounced = populations[int(OPPOSITE[lane])]
        pulled.append(jnp.where(in_domain, source, bounced))
        gas_side.append(in_domain & (source_flag < 0.5))
        weight = jnp.where(
            in_domain & (source_flag > 1.5),
            1.0,
            jnp.where(in_domain & (source_flag > 0.5), 0.5 * (fraction + source_fraction), 0.0),
        )
        mass_flux = mass_flux + weight * (source - bounced)
        targets = targets + jnp.where(in_domain & (jnp.abs(source_status - 1.0) < 0.5), 1.0, 0.0)
    return (jnp.stack(pulled), jnp.stack(gas_side), mass_flux, targets)


def settle_cells(
    pulled,
    gas_side,
    populations,
    velocity,
    local_gas,
    cell_mass,
    cell_flags,
    conversion,
    mass_flux,
    targets,
):
    unit = unit_equilibrium(velocity)
    paired = unit + unit[OPPOSITE]
    bounced = populations[OPPOSITE]
    wetted = cell_flags > 0
    passed = jnp.where(gas_side, local_gas[None] * paired - bounced, pulled)
    passed = jnp.where(wetted[None], passed, populations)
    moved_density, moved_velocity = moments(passed)
    relaxed = passed - RELAX * (passed - moved_density[None] * unit_equilibrium(moved_velocity))
    relaxed = jnp.where(wetted[None], relaxed, populations)
    filling = (cell_flags == 1) & (conversion == 1)
    updated = jnp.where(
        cell_flags == 1, cell_mass + mass_flux, jnp.where(cell_flags == 2, moved_density, cell_mass)
    )
    portion = jnp.where(filling, (updated - moved_density) / jnp.maximum(targets, 1.0), 0.0)
    updated = jnp.where(filling, moved_density, updated)
    return (relaxed, updated, portion)


def collect_spill(padded_portion, extent_rows, extent_cols):
    gained = jnp.zeros((extent_rows, extent_cols, padded_portion.shape[2]), jnp.float32)
    for lane in range(1, 19):
        gained = gained + window(padded_portion, lane, extent_rows, extent_cols)
    return gained


def tally_volume(contribution, bubble, count):
    labels = jnp.arange(count, dtype=jnp.int32)
    layer_terms = contribution.reshape(contribution.shape[0], -1)
    layer_labels = bubble.reshape(bubble.shape[0], -1)

    def accumulate(running, layer_pair):
        terms, cell_labels = layer_pair
        indicator = (cell_labels[:, None] == labels[None, :]).astype(jnp.float32)
        summed = jnp.dot(
            terms, indicator, precision=lax.Precision.HIGHEST, preferred_element_type=jnp.float32
        )
        return (running + summed, None)

    running, _ = lax.scan(accumulate, jnp.zeros((count,), jnp.float32), (layer_terms, layer_labels))
    return running


def spread_density(gas_density, bubble):
    labels = jnp.arange(gas_density.shape[0], dtype=jnp.int32)
    layer_labels = bubble.reshape(bubble.shape[0], -1)

    def lookup(cell_labels):
        indicator = (cell_labels[:, None] == labels[None, :]).astype(jnp.float32)
        return jnp.dot(
            indicator,
            gas_density,
            precision=lax.Precision.HIGHEST,
            preferred_element_type=jnp.float32,
        )

    return lax.map(lookup, layer_labels).reshape(bubble.shape)


def total_volume(partial_volume):
    return lax.psum(partial_volume, ("gx", "gy"))


def shards(populations, cell_mass, cell_flags, bubble, conversion, rest_volume):
    extent_rows, extent_cols, extent_depth = (
        populations.shape[1],
        populations.shape[2],
        populations.shape[3],
    )
    density, velocity = moments(populations)
    fraction = jnp.clip(cell_mass / density, 0.0, 1.0)
    status = jnp.where((cell_flags == 1) & (conversion == 1), 4, cell_flags).astype(jnp.float32)
    contribution = jnp.where(cell_flags == 0, 1.0, jnp.where(cell_flags == 1, 1.0 - fraction, 0.0))
    partial_volume = tally_volume(contribution, bubble, rest_volume.shape[0])
    volume = total_volume(partial_volume)
    channels = jnp.concatenate([populations, fraction[None], status[None]], axis=0)
    padded = padded_2(channels, (("gx", 1), ("gy", 2)), 1)
    start_rows = lax.axis_index("gx") * extent_rows + jnp.arange(
        -1, extent_rows + 1, dtype=jnp.int32
    )
    start_cols = lax.axis_index("gy") * extent_cols + jnp.arange(
        -1, extent_cols + 1, dtype=jnp.int32
    )
    inside_rows = (start_rows >= 0) & (start_rows < extent_rows * lax.axis_size("gx"))
    inside_cols = (start_cols >= 0) & (start_cols < extent_cols * lax.axis_size("gy"))
    pulled, gas_side, mass_flux, targets = pull_cells(
        padded, inside_rows, inside_cols, populations, fraction
    )
    gas_density = AMBIENT + rest_volume / jnp.maximum(volume, 1.0)
    local_gas = spread_density(gas_density, bubble)
    relaxed, updated, portion = settle_cells(
        pulled,
        gas_side,
        populations,
        velocity,
        local_gas,
        cell_mass,
        cell_flags,
        conversion,
        mass_flux,
        targets,
    )
    padded_portion = padded_2(portion, (("gx", 0), ("gy", 1)), 1)
    gained = collect_spill(padded_portion, extent_rows, extent_cols)
    receiver = (cell_flags == 1) & (conversion == 0)
    new_mass = jnp.where(receiver, updated + gained, updated)
    return (relaxed, new_mass, gas_density)


def solution(mesh):
    placed = (
        P(None, "gx", "gy", None),
        P("gx", "gy", None),
        P("gx", "gy", None),
        P("gx", "gy", None),
        P("gx", "gy", None),
        P(),
    )
    return jax.shard_map(
        shards,
        mesh=mesh,
        in_specs=placed,
        out_specs=(P(None, "gx", "gy", None), P("gx", "gy", None), P()),
        check_vma=False,
    )
```

profile of v0, /device:TPU:9, one launch (start us, length us, event | category | flops | bytes accessed | tf_op | source)
XLA Modules:
  0.0 112.9 jit_solution(17620983186998840845)
XLA Ops:
  0.6 1.1 reduce_sum.36
  1.8 0.8 convert_bitcast_fusion
  2.6 3.1 %collective-permute-start = (f32[21,1,8,128]{3,2,1,0:T(8,128)S(1)}, f32[21,1,8,128]{3,2,1,0:T(8,128)S(1)}, u32[]{:S(2)}, u32[]{:S(2)}) collective-permute-start(f32[21,1,8,128]{3,2,1,0:T(8,128)S(1)} %get-tuple-element.136), channel_id=1, source_target_pairs={{0,4},{4,8},{8,12},{12,16},{16,20},{20,24},{24,28},{1,5},{5,9},{9,... | collective-permute-start | bytes 258056 | tf_op jit(solution)/shard_map/ppermute | solution.py:44
  5.7 3.1 %collective-permute-start.1 = (f32[21,1,8,128]{3,2,1,0:T(8,128)S(1)}, f32[21,1,8,128]{3,2,1,0:T(8,128)S(1)}, u32[]{:S(2)}, u32[]{:S(2)}) collective-permute-start(f32[21,1,8,128]{3,2,1,0:T(8,128)S(1)} %get-tuple-element.137), channel_id=1, source_target_pairs={{4,0},{8,4},{12,8},{16,12},{20,16},{24,20},{28,24},{5,1},{9,5},{13... | collective-permute-start | bytes 258056 | tf_op jit(solution)/shard_map/ppermute | solution.py:46
  9.0 0.6 broadcast_compare_fusion.1
  9.8 0.6 copy-done.68
  10.4 0.6 multiply_reduce_fusion.1
  11.0 0.6 copy-done.66
  11.7 0.8 fusion.15
  12.6 0.7 copy-done.58
  13.3 2.5 %while.23 = (s32[]{:T(128)}, f32[96]{0:T(128)S(1)}, f32[6,1024]{1,0:T(8,128)S(1)}, s32[6,1024]{1,0:T(8,128)S(1)}, s32[]{:T(128)}, /*index=5*/s32[]{:T(128)}) while((s32[]{:T(128)}, f32[96]{0:T(128)S(1)}, f32[6,1024]{1,0:T(8,128)S(1)}, s32[6,1024]{1,0:T(8,128)S(1)}, s32[]{:T(128)}, /*index=5*/s32[]{:T(128)}) %tuple.207), condition=%wide.region_2.3_spmd.clone, body=%wide.region_1.2_spmd.clone.sunk | while | flops 1278147 | bytes 17367 | solution.py:161
  15.8 39.3 %psum.7 = f32[96]{0:T(128)S(1)} all-reduce(f32[96]{0:T(128)S(1)} %get-tuple-element.57), channel_id=1, replica_groups=mesh['gx'=8,'gy'=4] {'gx','gy'}, use_global_device_ids=true, to_apply=%region_3.4 | all-reduce | flops 96 | bytes 768 | tf_op jit(solution)/shard_map/psum | solution.py:182
  55.1 3.5 %while.22 = (s32[]{:T(128)}, f32[6,1024]{1,0:T(8,128)S(1)}, s32[6,1024]{1,0:T(8,128)S(1)}, f32[96]{0:T(128)S(1)}, s32[]{:T(128)}, /*index=5*/s32[]{:T(128)}) while((s32[]{:T(128)}, f32[6,1024]{1,0:T(8,128)S(1)}, s32[6,1024]{1,0:T(8,128)S(1)}, f32[96]{0:T(128)S(1)}, s32[]{:T(128)}, /*index=5*/s32[]{:T(128)}) %tuple.206), condition=%wide.region_5.6_spmd.clone, body=%wide.region_4.5_spmd.clone.sunk | while | flops 1277954 | bytes 25037 | solution.py:178
  59.1 0.7 broadcast_and_fusion.3
  59.8 0.6 gather_fusion.1
  60.4 0.6 gather_fusion
  61.2 5.3 %collective-permute-start.2 = (f32[21,8,1,128]{3,2,1,0:T(1,128)S(1)}, f32[21,8,1,128]{3,2,1,0:T(1,128)S(1)}, u32[]{:S(2)}, u32[]{:S(2)}) collective-permute-start(f32[21,8,1,128]{3,2,1,0:T(1,128)S(1)} %get-tuple-element.132), channel_id=1, source_target_pairs={{0,1},{1,2},{2,3},{4,5},{5,6},{6,7},{8,9},{9,10},{10,11},{12,13},{... | collective-permute-start | bytes 258056 | tf_op jit(solution)/shard_map/ppermute | solution.py:44
  66.4 1.9 %collective-permute-start.3 = (f32[21,8,1,128]{3,2,1,0:T(1,128)S(1)}, f32[21,8,1,128]{3,2,1,0:T(1,128)S(1)}, u32[]{:S(2)}, u32[]{:S(2)}) collective-permute-start(f32[21,8,1,128]{3,2,1,0:T(1,128)S(1)} %get-tuple-element.133), channel_id=1, source_target_pairs={{1,0},{2,1},{3,2},{5,4},{6,5},{7,6},{9,8},{10,9},{11,10},{13,12},{... | collective-permute-start | bytes 258056 | tf_op jit(solution)/shard_map/ppermute | solution.py:46
  68.4 3.9 %collective-permute-done.3 = f32[21,8,1,128]{3,2,1,0:T(1,128)S(1)} collective-permute-done((f32[21,8,1,128]{3,2,1,0:T(1,128)S(1)}, f32[21,8,1,128]{3,2,1,0:T(1,128)S(1)}, u32[]{:S(2)}, u32[]{:S(2)}) %collective-permute-start.3) | collective-permute-done | bytes 86048 | tf_op jit(solution)/shard_map/ppermute | solution.py:46
  72.3 0.8 fusion.207
  73.0 0.8 fusion.208
  73.8 0.8 fusion.185
  74.6 0.7 fusion.186
  76.4 0.7 copy-done.53
  77.1 0.7 copy-done.55
  78.0 0.7 copy-done.56
  78.8 0.7 copy-done.62
  79.6 0.7 copy-done.60
  80.3 0.6 copy-done.61
  81.0 0.6 copy-done.59
  81.8 0.7 fusion.180
  82.6 0.7 bitcast_select_fusion.6
  84.1 0.6 copy-done.13
  85.5 0.7 bitcast_select_fusion
  86.2 0.8 maximum_select_fusion.4
  87.0 0.7 maximum_select_fusion.8
  87.7 3.1 %stack.91 = f32[19,6,8,128]{3,0,2,1:T(8,128)S(1)} concatenate(f32[1,6,8,128]{3,0,2,1:T(1,128)} %bitcast.312, f32[1,6,8,128]{3,0,2,1:T(1,128)} %bitcast.316, f32[1,6,8,128]{3,0,2,1:T(1,128)} %bitcast.315, f32[1,6,8,128]{3,0,2,1:T(1,128)} %bitcast.322, f32[1,6,8,128]{3,0,2,1:T(1,128)} %bitcast.321, f32[1,6,8,128]{3,0,2,1:T(1,128)} %bitcast.325, f32[1,6,8,128]{3,0,2,1:T(1,128)} %bitcast.326, ...), dimensions={0} | concatenate | bytes 933888 | tf_op jit(solution)/shard_map/stack | solution.py:108
  91.2 1.5 %fusion.178 = (f32[6,8,128]{2,1,0:T(8,128)S(1)}, f32[19,6,8,128]{3,0,2,1:T(8,128)S(1)}) fusion(f32[19,6,8,128]{3,2,1,0:T(8,128)S(1)} %copy-done, f32[19,6,8,128]{3,0,2,1:T(8,128)S(1)} %stack.91, f32[19,6,8,128]{3,2,1,0:T(8,128)S(1)} %gather_fusion.1, f32[19,6,8,128]{3,0,2,1:T(8,128)S(1)} %fusion.15, f32[19,6,8,128]{3,2,1,0:T(8,128)S(1)} %gather_fusion, ...), kind=kLoop, calls=%fused_computation.443 | loop fusion | flops 694272 | bytes 2973696 | tf_op jit(solution)/shard_map/reduce_sum | solution.py:54
  93.4 1.7 %divide_select_fusion = (f32[6,8,128]{2,1,0:T(8,128)S(1)}, f32[6,8,128]{2,1,0:T(8,128)S(1)}) fusion(f32[6,8,128]{2,1,0:T(8,128)S(1)} %get-tuple-element.110, f32[8,10,128]{2,1,0:T(8,128)S(1)} %get-tuple-element.114, pred[6,8]{1,0:T(8,128)(4,1)} %get-tuple-element.290, pred[6,8]{1,0:T(8,128)(4,1)} %get-tuple-element.284, ...), kind=kLoop, calls=%fused_computation.340 | loop fusion | flops 2463744 | bytes 1941936 | tf_op jit(solution)/shard_map/jit(_where)/select_n | solution.py:136
  95.1 3.1 %collective-permute-start.4 = (f32[1,8,128]{2,1,0:T(8,128)S(1)}, f32[1,8,128]{2,1,0:T(8,128)S(1)}, u32[]{:S(2)}, u32[]{:S(2)}) collective-permute-start(f32[1,8,128]{2,1,0:T(8,128)S(1)} %get-tuple-element.282), channel_id=1, source_target_pairs={{0,4},{4,8},{8,12},{12,16},{16,20},{20,24},{24,28},{1,5},{5,9},{9,... | collective-permute-start | bytes 12296 | tf_op jit(solution)/shard_map/ppermute | solution.py:44
  98.3 3.1 %collective-permute-start.5 = (f32[1,8,128]{2,1,0:T(8,128)S(1)}, f32[1,8,128]{2,1,0:T(8,128)S(1)}, u32[]{:S(2)}, u32[]{:S(2)}) collective-permute-start(f32[1,8,128]{2,1,0:T(8,128)S(1)} %get-tuple-element.283), channel_id=1, source_target_pairs={{4,0},{8,4},{12,8},{16,12},{20,16},{24,20},{28,24},{5,1},{9,5},{13... | collective-permute-start | bytes 12296 | tf_op jit(solution)/shard_map/ppermute | solution.py:46
  101.9 0.6 copy-done.57
  102.6 1.0 fusion.23
  103.6 0.9 copy.112
  104.4 2.4 %collective-permute-start.6 = (f32[8,1,128]{2,1,0:T(1,128)S(1)}, f32[8,1,128]{2,1,0:T(1,128)S(1)}, u32[]{:S(2)}, u32[]{:S(2)}) collective-permute-start(f32[8,1,128]{2,1,0:T(1,128)S(1)} %get-tuple-element.271), channel_id=1, source_target_pairs={{0,1},{1,2},{2,3},{4,5},{5,6},{6,7},{8,9},{9,10},{10,11},{12,13},{... | collective-permute-start | bytes 12296 | tf_op jit(solution)/shard_map/ppermute | solution.py:44
  106.9 1.9 %collective-permute-start.7 = (f32[8,1,128]{2,1,0:T(1,128)S(1)}, f32[8,1,128]{2,1,0:T(1,128)S(1)}, u32[]{:S(2)}, u32[]{:S(2)}) collective-permute-start(f32[8,1,128]{2,1,0:T(1,128)S(1)} %get-tuple-element.270), channel_id=1, source_target_pairs={{1,0},{2,1},{3,2},{5,4},{6,5},{7,6},{9,8},{10,9},{11,10},{13,12},{... | collective-permute-start | bytes 12296 | tf_op jit(solution)/shard_map/ppermute | solution.py:46
  109.0 2.8 %collective-permute-done.7 = f32[8,1,128]{2,1,0:T(1,128)S(1)} collective-permute-done((f32[8,1,128]{2,1,0:T(1,128)S(1)}, f32[8,1,128]{2,1,0:T(1,128)S(1)}, u32[]{:S(2)}, u32[]{:S(2)}) %collective-permute-start.7) | collective-permute-done | bytes 4128 | tf_op jit(solution)/shard_map/ppermute | solution.py:46
  112.1 0.8 add_select_fusion
  (238 shorter events, 11.7 us)
Async XLA Ops:
  0.6 2.0 %copy-start = (f32[19,6,8,128]{3,2,1,0:T(8,128)S(1)}, f32[19,6,8,128]{3,2,1,0:T(8,128)}, u32[]{:S(2)}) copy-start(f32[19,6,8,128]{3,2,1,0:T(8,128)} %param.19) | copy-start | bytes 1400836
  1.8 8.0 %copy-start.3 = (f32[6,8,128]{2,1,0:T(8,128)}, f32[6,8,128]{2,1,0:T(8,128)S(1)}, u32[]{:S(2)}) copy-start(f32[6,8,128]{2,1,0:T(8,128)S(1)} %reduce_sum.36) | copy-start | bytes 73732
  2.6 58.4 %collective-permute-start = (f32[21,1,8,128]{3,2,1,0:T(8,128)S(1)}, f32[21,1,8,128]{3,2,1,0:T(8,128)S(1)}, u32[]{:S(2)}, u32[]{:S(2)}) collective-permute-start(f32[21,1,8,128]{3,2,1,0:T(8,128)S(1)} %get-tuple-element.136), channel_id=1, source_target_pairs={{0,4},{4,8},{8,12},{12,16},{16,20},{20,24},{24,28},{1,5},{5,9},{9,... | collective-permute-start | bytes 258056 | tf_op jit(solution)/shard_map/ppermute | solution.py:44
  5.7 55.3 %collective-permute-start.1 = (f32[21,1,8,128]{3,2,1,0:T(8,128)S(1)}, f32[21,1,8,128]{3,2,1,0:T(8,128)S(1)}, u32[]{:S(2)}, u32[]{:S(2)}) collective-permute-start(f32[21,1,8,128]{3,2,1,0:T(8,128)S(1)} %get-tuple-element.137), channel_id=1, source_target_pairs={{4,0},{8,4},{12,8},{16,12},{20,16},{24,20},{28,24},{5,1},{9,5},{13... | collective-permute-start | bytes 258056 | tf_op jit(solution)/shard_map/ppermute | solution.py:46
  15.8 39.3 %copy-start.64 = (f32[96]{0:T(128)S(1)}, f32[96]{0:T(128)}, u32[]{:S(2)}) copy-start(f32[96]{0:T(128)} %param.24) | copy-start | bytes 1156
  61.2 7.2 %collective-permute-start.2 = (f32[21,8,1,128]{3,2,1,0:T(1,128)S(1)}, f32[21,8,1,128]{3,2,1,0:T(1,128)S(1)}, u32[]{:S(2)}, u32[]{:S(2)}) collective-permute-start(f32[21,8,1,128]{3,2,1,0:T(1,128)S(1)} %get-tuple-element.132), channel_id=1, source_target_pairs={{0,1},{1,2},{2,3},{4,5},{5,6},{6,7},{8,9},{9,10},{10,11},{12,13},{... | collective-permute-start | bytes 258056 | tf_op jit(solution)/shard_map/ppermute | solution.py:44
  66.4 5.8 %collective-permute-start.3 = (f32[21,8,1,128]{3,2,1,0:T(1,128)S(1)}, f32[21,8,1,128]{3,2,1,0:T(1,128)S(1)}, u32[]{:S(2)}, u32[]{:S(2)}) collective-permute-start(f32[21,8,1,128]{3,2,1,0:T(1,128)S(1)} %get-tuple-element.133), channel_id=1, source_target_pairs={{1,0},{2,1},{3,2},{5,4},{6,5},{7,6},{9,8},{10,9},{11,10},{13,12},{... | collective-permute-start | bytes 258056 | tf_op jit(solution)/shard_map/ppermute | solution.py:46
  87.7 3.1 %copy-start.14 = (pred[19,6,8,128]{3,2,1,0:T(8,128)(4,1)S(1)}, pred[19,6,8,128]{3,2,1,0:T(8,128)(4,1)}, u32[]{:S(2)}) copy-start(pred[19,6,8,128]{3,2,1,0:T(8,128)(4,1)} %copy-done.13) | copy-start | bytes 350212
  90.8 1.9 %copy-start.16 = (f32[6,8,1]{2,1,0:T(8,128)S(1)}, f32[6,8,1]{2,1,0:T(8,128)}, u32[]{:S(2)}) copy-start(f32[6,8,1]{2,1,0:T(8,128)} %get-tuple-element.239) | copy-start | bytes 580
  90.8 1.9 %copy-start.17 = (f32[6,8,1]{2,1,0:T(8,128)S(1)}, f32[6,8,1]{2,1,0:T(8,128)}, u32[]{:S(2)}) copy-start(f32[6,8,1]{2,1,0:T(8,128)} %get-tuple-element.240) | copy-start | bytes 580
  90.8 1.9 %copy-start.18 = (f32[6,8,1]{2,1,0:T(8,128)S(1)}, f32[6,8,1]{2,1,0:T(8,128)}, u32[]{:S(2)}) copy-start(f32[6,8,1]{2,1,0:T(8,128)} %get-tuple-element.241) | copy-start | bytes 580
  90.8 1.9 %copy-start.19 = (f32[6,8,1]{2,1,0:T(8,128)S(1)}, f32[6,8,1]{2,1,0:T(8,128)}, u32[]{:S(2)}) copy-start(f32[6,8,1]{2,1,0:T(8,128)} %get-tuple-element.242) | copy-start | bytes 580
  90.9 1.9 %copy-start.20 = (f32[6,8,1]{2,1,0:T(8,128)S(1)}, f32[6,8,1]{2,1,0:T(8,128)}, u32[]{:S(2)}) copy-start(f32[6,8,1]{2,1,0:T(8,128)} %get-tuple-element.243) | copy-start | bytes 580
  90.9 1.9 %copy-start.21 = (f32[6,8,1]{2,1,0:T(8,128)S(1)}, f32[6,8,1]{2,1,0:T(8,128)}, u32[]{:S(2)}) copy-start(f32[6,8,1]{2,1,0:T(8,128)} %get-tuple-element.244) | copy-start | bytes 580
  90.9 1.9 %copy-start.22 = (f32[6,8,1]{2,1,0:T(8,128)S(1)}, f32[6,8,1]{2,1,0:T(8,128)}, u32[]{:S(2)}) copy-start(f32[6,8,1]{2,1,0:T(8,128)} %get-tuple-element.245) | copy-start | bytes 580
  90.9 1.9 %copy-start.23 = (f32[6,8,1]{2,1,0:T(8,128)S(1)}, f32[6,8,1]{2,1,0:T(8,128)}, u32[]{:S(2)}) copy-start(f32[6,8,1]{2,1,0:T(8,128)} %get-tuple-element.246) | copy-start | bytes 580
  90.9 1.9 %copy-start.24 = (f32[6,8,127]{2,1,0:T(8,128)S(1)}, f32[6,8,127]{2,1,0:T(8,128)}, u32[]{:S(2)}) copy-start(f32[6,8,127]{2,1,0:T(8,128)} %get-tuple-element.247) | copy-start | bytes 73156
  90.9 1.9 %copy-start.25 = (f32[6,8,127]{2,1,0:T(8,128)S(1)}, f32[6,8,127]{2,1,0:T(8,128)}, u32[]{:S(2)}) copy-start(f32[6,8,127]{2,1,0:T(8,128)} %get-tuple-element.258) | copy-start | bytes 73156
  90.9 1.9 %copy-start.26 = (f32[6,8,127]{2,1,0:T(8,128)S(1)}, f32[6,8,127]{2,1,0:T(8,128)}, u32[]{:S(2)}) copy-start(f32[6,8,127]{2,1,0:T(8,128)} %get-tuple-element.259) | copy-start | bytes 73156
  90.9 1.9 %copy-start.27 = (f32[6,8,127]{2,1,0:T(8,128)S(1)}, f32[6,8,127]{2,1,0:T(8,128)}, u32[]{:S(2)}) copy-start(f32[6,8,127]{2,1,0:T(8,128)} %get-tuple-element.260) | copy-start | bytes 73156
  90.9 1.9 %copy-start.28 = (f32[6,8,127]{2,1,0:T(8,128)S(1)}, f32[6,8,127]{2,1,0:T(8,128)}, u32[]{:S(2)}) copy-start(f32[6,8,127]{2,1,0:T(8,128)} %get-tuple-element.261) | copy-start | bytes 73156
  90.9 1.9 %copy-start.29 = (f32[6,8,127]{2,1,0:T(8,128)S(1)}, f32[6,8,127]{2,1,0:T(8,128)}, u32[]{:S(2)}) copy-start(f32[6,8,127]{2,1,0:T(8,128)} %get-tuple-element.262) | copy-start | bytes 73156
  91.0 1.9 %copy-start.30 = (f32[6,8,127]{2,1,0:T(8,128)S(1)}, f32[6,8,127]{2,1,0:T(8,128)}, u32[]{:S(2)}) copy-start(f32[6,8,127]{2,1,0:T(8,128)} %get-tuple-element.263) | copy-start | bytes 73156
  91.0 1.9 %copy-start.31 = (f32[6,8,127]{2,1,0:T(8,128)S(1)}, f32[6,8,127]{2,1,0:T(8,128)}, u32[]{:S(2)}) copy-start(f32[6,8,127]{2,1,0:T(8,128)} %get-tuple-element.264) | copy-start | bytes 73156
  91.0 1.9 %copy-start.32 = (f32[6,8,127]{2,1,0:T(8,128)S(1)}, f32[6,8,127]{2,1,0:T(8,128)}, u32[]{:S(2)}) copy-start(f32[6,8,127]{2,1,0:T(8,128)} %get-tuple-element.265) | copy-start | bytes 73156
  91.0 1.9 %copy-start.33 = (f32[6,8,1]{2,1,0:T(8,128)S(1)}, f32[6,8,1]{2,1,0:T(8,128)}, u32[]{:S(2)}) copy-start(f32[6,8,1]{2,1,0:T(8,128)} %get-tuple-element.168) | copy-start | bytes 580
  91.0 1.9 %copy-start.34 = (f32[6,8,1]{2,1,0:T(8,128)S(1)}, f32[6,8,1]{2,1,0:T(8,128)}, u32[]{:S(2)}) copy-start(f32[6,8,1]{2,1,0:T(8,128)} %get-tuple-element.169) | copy-start | bytes 580
  91.0 1.9 %copy-start.35 = (f32[6,8,1]{2,1,0:T(8,128)S(1)}, f32[6,8,1]{2,1,0:T(8,128)}, u32[]{:S(2)}) copy-start(f32[6,8,1]{2,1,0:T(8,128)} %get-tuple-element.170) | copy-start | bytes 580
  91.0 1.9 %copy-start.36 = (f32[6,8,1]{2,1,0:T(8,128)S(1)}, f32[6,8,1]{2,1,0:T(8,128)}, u32[]{:S(2)}) copy-start(f32[6,8,1]{2,1,0:T(8,128)} %get-tuple-element.171) | copy-start | bytes 580
  91.0 1.9 %copy-start.37 = (f32[6,8,1]{2,1,0:T(8,128)S(1)}, f32[6,8,1]{2,1,0:T(8,128)}, u32[]{:S(2)}) copy-start(f32[6,8,1]{2,1,0:T(8,128)} %get-tuple-element.172) | copy-start | bytes 580
  91.0 1.9 %copy-start.38 = (f32[6,8,1]{2,1,0:T(8,128)S(1)}, f32[6,8,1]{2,1,0:T(8,128)}, u32[]{:S(2)}) copy-start(f32[6,8,1]{2,1,0:T(8,128)} %get-tuple-element.173) | copy-start | bytes 580
  91.0 1.9 %copy-start.39 = (f32[6,8,1]{2,1,0:T(8,128)S(1)}, f32[6,8,1]{2,1,0:T(8,128)}, u32[]{:S(2)}) copy-start(f32[6,8,1]{2,1,0:T(8,128)} %get-tuple-element.174) | copy-start | bytes 580
  91.1 1.9 %copy-start.40 = (f32[6,8,1]{2,1,0:T(8,128)S(1)}, f32[6,8,1]{2,1,0:T(8,128)}, u32[]{:S(2)}) copy-start(f32[6,8,1]{2,1,0:T(8,128)} %get-tuple-element.175) | copy-start | bytes 580
  91.1 1.9 %copy-start.41 = (f32[6,8,1]{2,1,0:T(8,128)S(1)}, f32[6,8,1]{2,1,0:T(8,128)}, u32[]{:S(2)}) copy-start(f32[6,8,1]{2,1,0:T(8,128)} %get-tuple-element.176) | copy-start | bytes 580
  91.1 1.9 %copy-start.42 = (f32[6,8,1]{2,1,0:T(8,128)S(1)}, f32[6,8,1]{2,1,0:T(8,128)}, u32[]{:S(2)}) copy-start(f32[6,8,1]{2,1,0:T(8,128)} %get-tuple-element.177) | copy-start | bytes 580
  91.1 1.9 %copy-start.43 = (f32[6,8,1]{2,1,0:T(8,128)S(1)}, f32[6,8,1]{2,1,0:T(8,128)}, u32[]{:S(2)}) copy-start(f32[6,8,1]{2,1,0:T(8,128)} %get-tuple-element.320) | copy-start | bytes 580
  91.1 1.9 %copy-start.44 = (f32[6,8,127]{2,1,0:T(8,128)S(1)}, f32[6,8,127]{2,1,0:T(8,128)}, u32[]{:S(2)}) copy-start(f32[6,8,127]{2,1,0:T(8,128)} %get-tuple-element.178) | copy-start | bytes 73156
  91.1 1.9 %copy-start.45 = (f32[6,8,127]{2,1,0:T(8,128)S(1)}, f32[6,8,127]{2,1,0:T(8,128)}, u32[]{:S(2)}) copy-start(f32[6,8,127]{2,1,0:T(8,128)} %get-tuple-element.179) | copy-start | bytes 73156
  91.1 1.9 %copy-start.46 = (f32[6,8,127]{2,1,0:T(8,128)S(1)}, f32[6,8,127]{2,1,0:T(8,128)}, u32[]{:S(2)}) copy-start(f32[6,8,127]{2,1,0:T(8,128)} %get-tuple-element.180) | copy-start | bytes 73156
  91.1 1.9 %copy-start.47 = (f32[6,8,127]{2,1,0:T(8,128)S(1)}, f32[6,8,127]{2,1,0:T(8,128)}, u32[]{:S(2)}) copy-start(f32[6,8,127]{2,1,0:T(8,128)} %get-tuple-element.181) | copy-start | bytes 73156
  91.1 1.9 %copy-start.48 = (f32[6,8,127]{2,1,0:T(8,128)S(1)}, f32[6,8,127]{2,1,0:T(8,128)}, u32[]{:S(2)}) copy-start(f32[6,8,127]{2,1,0:T(8,128)} %get-tuple-element.182) | copy-start | bytes 73156
  91.1 1.9 %copy-start.49 = (f32[6,8,127]{2,1,0:T(8,128)S(1)}, f32[6,8,127]{2,1,0:T(8,128)}, u32[]{:S(2)}) copy-start(f32[6,8,127]{2,1,0:T(8,128)} %get-tuple-element.183) | copy-start | bytes 73156
  91.2 1.9 %copy-start.50 = (f32[6,8,127]{2,1,0:T(8,128)S(1)}, f32[6,8,127]{2,1,0:T(8,128)}, u32[]{:S(2)}) copy-start(f32[6,8,127]{2,1,0:T(8,128)} %get-tuple-element.184) | copy-start | bytes 73156
  95.1 6.2 %copy-start.69 = (f32[3,19,1,1]{1,0,3,2:T(4,128)S(1)}, f32[3,19,1,1]{1,0,3,2:T(4,128)}, u32[]{:S(2)}) copy-start(f32[3,19,1,1]{1,0,3,2:T(4,128)} %constant.139) | copy-start | bytes 688
  95.1 9.3 %collective-permute-start.4 = (f32[1,8,128]{2,1,0:T(8,128)S(1)}, f32[1,8,128]{2,1,0:T(8,128)S(1)}, u32[]{:S(2)}, u32[]{:S(2)}) collective-permute-start(f32[1,8,128]{2,1,0:T(8,128)S(1)} %get-tuple-element.282), channel_id=1, source_target_pairs={{0,4},{4,8},{8,12},{12,16},{16,20},{20,24},{24,28},{1,5},{5,9},{9,... | collective-permute-start | bytes 12296 | tf_op jit(solution)/shard_map/ppermute | solution.py:44
  98.3 6.2 %collective-permute-start.5 = (f32[1,8,128]{2,1,0:T(8,128)S(1)}, f32[1,8,128]{2,1,0:T(8,128)S(1)}, u32[]{:S(2)}, u32[]{:S(2)}) collective-permute-start(f32[1,8,128]{2,1,0:T(8,128)S(1)} %get-tuple-element.283), channel_id=1, source_target_pairs={{4,0},{8,4},{12,8},{16,12},{20,16},{24,20},{28,24},{5,1},{9,5},{13... | collective-permute-start | bytes 12296 | tf_op jit(solution)/shard_map/ppermute | solution.py:46
  104.4 4.5 %collective-permute-start.6 = (f32[8,1,128]{2,1,0:T(1,128)S(1)}, f32[8,1,128]{2,1,0:T(1,128)S(1)}, u32[]{:S(2)}, u32[]{:S(2)}) collective-permute-start(f32[8,1,128]{2,1,0:T(1,128)S(1)} %get-tuple-element.271), channel_id=1, source_target_pairs={{0,1},{1,2},{2,3},{4,5},{5,6},{6,7},{8,9},{9,10},{10,11},{12,13},{... | collective-permute-start | bytes 12296 | tf_op jit(solution)/shard_map/ppermute | solution.py:44
  106.9 4.9 %collective-permute-start.7 = (f32[8,1,128]{2,1,0:T(1,128)S(1)}, f32[8,1,128]{2,1,0:T(1,128)S(1)}, u32[]{:S(2)}, u32[]{:S(2)}) collective-permute-start(f32[8,1,128]{2,1,0:T(1,128)S(1)} %get-tuple-element.270), channel_id=1, source_target_pairs={{1,0},{2,1},{3,2},{5,4},{6,5},{7,6},{9,8},{10,9},{11,10},{13,12},{... | collective-permute-start | bytes 12296 | tf_op jit(solution)/shard_map/ppermute | solution.py:46
  (32 other events, 24.7 us)
where the time goes:
time: 114 us; the launch traced here: 113 us
  blocking collectives  39.3 us (34%)
  starting transfers between devices  23.9 us (21%)
  local copies, waits for them, and re-layouts  19.9 us (17%)
  other arithmetic  13 us (11%)
  matrix products  7.83 us (7%)
  waiting for transfers between devices  6.69 us (6%)
  between operations  1.85 us (2%)
    psum x1, blocking collectives, total_volume(): return lax.psum(partial_volume, ('gx', 'gy'))  39.3 us
    ppermute x4, starting transfers between devices, padded_2(): lax.ppermute(tail, axis, [(i, (i + 1) % count) for i in range(ends)])  13.9 us
    unnamed x150, local copies, waits for them, and re-layouts  10.6 us
    ppermute x4, starting transfers between devices, padded_2(): lax.ppermute(head, axis, [((i + 1) % count, i) for i in range(ends)])  9.98 us
    ppermute x4, waiting for transfers between devices, padded_2(): lax.ppermute(head, axis, [((i + 1) % count, i) for i in range(ends)])  6.68 us
    slice x20, local copies, waits for them, and re-layouts, window(): jnp.roll(layer[begin_rows:begin_rows + extent_rows, begin_cols:begin_cols...  4.09 us
    another operation x1, local copies, waits for them, and re-layouts, pull_cells(): return (jnp.stack(pulled), jnp.stack(gas_side), mass_flux, targets)  3.12 us
    select_n x4, other arithmetic, pull_cells(): pulled.append(jnp.where(in_domain, source, bounced))  2.9 us
  transfers between devices with their start and end apart: 8, of which 2 were waited for; matrix products, arithmetic and copies ran while one was open for 11% of the time, Pallas kernels for 0%

commit v1 on v0

--- a/solution.py
+++ b/solution.py
@@ -179,7 +179,8 @@
 
 
 def total_volume(partial_volume):
-    return lax.psum(partial_volume, ("gx", "gy"))
+    cycles_time = lambda content, bus_axis: lax.all_gather(content, bus_axis).sum(axis=0)
+    return cycles_time(partial_volume, ("gx", "gy"))
 
 
 def shards(populations, cell_mass, cell_flags, bubble, conversion, rest_volume):

time: 114 us -> 118 us (1.035)
  local copies, waits for them, and re-layouts: 19.9 us -> 23.9 us
    unnamed x0 -> x1, blocking collectives: none -> 39.4 us
    psum x1 -> x0, blocking collectives: 39.3 us -> none  [total_volume(): return lax.psum(partial_volume, ('gx', 'gy'))]
    slice x20, local copies, waits for them, and re-layouts: 4.09 us -> 7.1 us  [window(): jnp.roll(layer[begin_rows:begin_rows + extent_rows, begin_cols:begin_cols...]
    unnamed x150 -> x154, local copies, waits for them, and re-layouts: 10.6 us -> 11.6 us
where the time goes in v1:
time: 118 us; the launch traced here: 117 us
  blocking collectives  39.4 us (33%)
  local copies, waits for them, and re-layouts  23.9 us (20%)
  starting transfers between devices  23.9 us (20%)
  other arithmetic  12.6 us (11%)
  matrix products  7.83 us (7%)
  waiting for transfers between devices  6.69 us (6%)
  between operations  1.89 us (2%)
    unnamed x1, blocking collectives  39.4 us
    ppermute x4, starting transfers between devices, padded_2(): lax.ppermute(tail, axis, [(i, (i + 1) % count) for i in range(ends)])  13.9 us
    unnamed x154, local copies, waits for them, and re-layouts  11.6 us
    ppermute x4, starting transfers between devices, padded_2(): lax.ppermute(head, axis, [((i + 1) % count, i) for i in range(ends)])  9.98 us
    slice x20, local copies, waits for them, and re-layouts, window(): jnp.roll(layer[begin_rows:begin_rows + extent_rows, begin_cols:begin_cols...  7.1 us
    ppermute x4, waiting for transfers between devices, padded_2(): lax.ppermute(head, axis, [((i + 1) % count, i) for i in range(ends)])  6.68 us
    another operation x1, local copies, waits for them, and re-layouts, pull_cells(): return (jnp.stack(pulled), jnp.stack(gas_side), mass_flux, targets)  3.03 us
    dot_general x6, matrix products, lookup(): jnp.dot(indicator, gas_density, precision=lax.Precision.HIGHEST, preferre...  2.66 us
  transfers between devices with their start and end apart: 8, of which 2 were waited for; matrix products, arithmetic and copies ran while one was open for 11% of the time, Pallas kernels for 0%

profile of v1, /device:TPU:9, one launch (start us, length us, event | category | flops | bytes accessed | tf_op | source)
XLA Modules:
  0.0 116.5 jit_solution(7284970047253422985)
XLA Ops:
  0.6 1.1 reduce_sum.45
  1.8 0.8 convert_bitcast_fusion
  2.6 3.1 %collective-permute-start = (f32[21,1,8,128]{3,2,1,0:T(8,128)S(1)}, f32[21,1,8,128]{3,2,1,0:T(8,128)S(1)}, u32[]{:S(2)}, u32[]{:S(2)}) collective-permute-start(f32[21,1,8,128]{3,2,1,0:T(8,128)S(1)} %get-tuple-element.139), channel_id=1, source_target_pairs={{0,4},{4,8},{8,12},{12,16},{16,20},{20,24},{24,28},{1,5},{5,9},{9,... | collective-permute-start | bytes 258056 | tf_op jit(solution)/shard_map/ppermute | solution.py:44
  5.7 3.1 %collective-permute-start.1 = (f32[21,1,8,128]{3,2,1,0:T(8,128)S(1)}, f32[21,1,8,128]{3,2,1,0:T(8,128)S(1)}, u32[]{:S(2)}, u32[]{:S(2)}) collective-permute-start(f32[21,1,8,128]{3,2,1,0:T(8,128)S(1)} %get-tuple-element.140), channel_id=1, source_target_pairs={{4,0},{8,4},{12,8},{16,12},{20,16},{24,20},{28,24},{5,1},{9,5},{13... | collective-permute-start | bytes 258056 | tf_op jit(solution)/shard_map/ppermute | solution.py:46
  11.0 0.6 copy-done.67
  11.7 0.8 fusion.15
  12.6 0.7 copy-done.59
  13.3 2.5 %while.23 = (s32[]{:T(128)}, f32[96]{0:T(128)S(1)}, f32[6,1024]{1,0:T(8,128)S(1)}, s32[6,1024]{1,0:T(8,128)S(1)}, s32[]{:T(128)}, /*index=5*/s32[]{:T(128)}) while((s32[]{:T(128)}, f32[96]{0:T(128)S(1)}, f32[6,1024]{1,0:T(8,128)S(1)}, s32[6,1024]{1,0:T(8,128)S(1)}, s32[]{:T(128)}, /*index=5*/s32[]{:T(128)}) %tuple.208), condition=%wide.region_2.3_spmd.clone, body=%wide.region_1.2_spmd.clone.sunk | while | flops 1278147 | bytes 17367 | solution.py:161
  16.1 39.4 %all-reduce = f32[3072]{0:T(1024)S(1)} all-reduce(f32[3072]{0:T(1024)S(1)} %dynamic-update-slice), channel_id=2, replica_groups=mesh['gx'=8,'gy'=4] {'gx','gy'}, use_global_device_ids=true, to_apply=%add | all-reduce | flops 3072 | bytes 24576
  55.6 0.6 copy-done.65
  56.2 3.5 %while.22 = (s32[]{:T(128)}, f32[6,1024]{1,0:T(8,128)S(1)}, s32[6,1024]{1,0:T(8,128)S(1)}, f32[96]{0:T(128)S(1)}, s32[]{:T(128)}, /*index=5*/s32[]{:T(128)}) while((s32[]{:T(128)}, f32[6,1024]{1,0:T(8,128)S(1)}, s32[6,1024]{1,0:T(8,128)S(1)}, f32[96]{0:T(128)S(1)}, s32[]{:T(128)}, /*index=5*/s32[]{:T(128)}) %tuple.207), condition=%wide.region_5.6_spmd.clone, body=%wide.region_4.5_spmd.clone.sunk | while | flops 1277954 | bytes 25037 | solution.py:178
  60.2 0.7 broadcast_and_fusion.3
  62.3 5.3 %collective-permute-start.2 = (f32[21,8,1,128]{3,2,1,0:T(1,128)S(1)}, f32[21,8,1,128]{3,2,1,0:T(1,128)S(1)}, u32[]{:S(2)}, u32[]{:S(2)}) collective-permute-start(f32[21,8,1,128]{3,2,1,0:T(1,128)S(1)} %get-tuple-element.135), channel_id=1, source_target_pairs={{0,1},{1,2},{2,3},{4,5},{5,6},{6,7},{8,9},{9,10},{10,11},{12,13},{... | collective-permute-start | bytes 258056 | tf_op jit(solution)/shard_map/ppermute | solution.py:44
  67.6 1.9 %collective-permute-start.3 = (f32[21,8,1,128]{3,2,1,0:T(1,128)S(1)}, f32[21,8,1,128]{3,2,1,0:T(1,128)S(1)}, u32[]{:S(2)}, u32[]{:S(2)}) collective-permute-start(f32[21,8,1,128]{3,2,1,0:T(1,128)S(1)} %get-tuple-element.136), channel_id=1, source_target_pairs={{1,0},{2,1},{3,2},{5,4},{6,5},{7,6},{9,8},{10,9},{11,10},{13,12},{... | collective-permute-start | bytes 258056 | tf_op jit(solution)/shard_map/ppermute | solution.py:46
  69.5 3.9 %collective-permute-done.3 = f32[21,8,1,128]{3,2,1,0:T(1,128)S(1)} collective-permute-done((f32[21,8,1,128]{3,2,1,0:T(1,128)S(1)}, f32[21,8,1,128]{3,2,1,0:T(1,128)S(1)}, u32[]{:S(2)}, u32[]{:S(2)}) %collective-permute-start.3) | collective-permute-done | bytes 86048 | tf_op jit(solution)/shard_map/ppermute | solution.py:46
  73.4 0.8 fusion.207
  74.2 0.8 fusion.208
  75.0 0.8 fusion.185
  75.7 0.7 fusion.186
  77.1 0.7 fusion.200
  77.8 0.7 fusion.203
  78.5 0.6 fusion.204
  79.1 0.7 slice.860
  79.8 0.6 slice.861
  80.6 0.6 copy-done.55
  81.4 0.7 copy-done.57
  82.2 0.7 copy-done.63
  83.0 0.7 copy-done.61
  83.7 0.7 copy-done.62
  84.5 0.6 copy-done.60
  85.3 0.7 fusion.180
  86.1 0.7 bitcast_select_fusion.6
  87.6 0.6 copy-done.13
  88.9 0.7 bitcast_select_fusion
  89.7 0.8 maximum_select_fusion.4
  90.6 0.7 copy-done.54
  91.3 3.0 %stack.91 = f32[19,6,8,128]{3,0,2,1:T(8,128)S(1)} concatenate(f32[1,6,8,128]{3,0,2,1:T(1,128)S(1)} %bitcast.312, f32[1,6,8,128]{3,0,2,1:T(1,128)S(1)} %bitcast.316, f32[1,6,8,128]{3,0,2,1:T(1,128)S(1)} %bitcast.315, f32[1,6,8,128]{3,0,2,1:T(1,128)} %bitcast.322, f32[1,6,8,128]{3,0,2,1:T(1,128)} %bitcast.321, f32[1,6,8,128]{3,0,2,1:T(1,128)} %bitcast.325, ...), dimensions={0} | concatenate | bytes 933888 | tf_op jit(solution)/shard_map/stack | solution.py:108
  94.7 1.5 %fusion.178 = (f32[6,8,128]{2,1,0:T(8,128)S(1)}, f32[19,6,8,128]{3,0,2,1:T(8,128)S(1)}) fusion(f32[19,6,8,128]{3,2,1,0:T(8,128)S(1)} %copy-done, f32[19,6,8,128]{3,0,2,1:T(8,128)S(1)} %stack.91, f32[19,6,8,128]{3,2,1,0:T(8,128)S(1)} %gather_fusion.1, f32[19,6,8,128]{3,0,2,1:T(8,128)S(1)} %fusion.15, f32[19,6,8,128]{3,2,1,0:T(8,128)S(1)} %gather_fusion, ...), kind=kLoop, calls=%fused_computation.443 | loop fusion | flops 694272 | bytes 2973696 | tf_op jit(solution)/shard_map/reduce_sum | solution.py:54
  97.0 1.8 %divide_select_fusion = (f32[6,8,128]{2,1,0:T(8,128)S(1)}, f32[6,8,128]{2,1,0:T(8,128)S(1)}) fusion(f32[6,8,128]{2,1,0:T(8,128)S(1)} %get-tuple-element.113, f32[8,10,128]{2,1,0:T(8,128)S(1)} %get-tuple-element.117, pred[6,8]{1,0:T(8,128)(4,1)} %get-tuple-element.293, pred[6,8]{1,0:T(8,128)(4,1)} %get-tuple-element.287, ...), kind=kLoop, calls=%fused_computation.340 | loop fusion | flops 2463744 | bytes 1941936 | tf_op jit(solution)/shard_map/jit(_where)/select_n | solution.py:136
  98.8 3.1 %collective-permute-start.4 = (f32[1,8,128]{2,1,0:T(8,128)S(1)}, f32[1,8,128]{2,1,0:T(8,128)S(1)}, u32[]{:S(2)}, u32[]{:S(2)}) collective-permute-start(f32[1,8,128]{2,1,0:T(8,128)S(1)} %get-tuple-element.285), channel_id=1, source_target_pairs={{0,4},{4,8},{8,12},{12,16},{16,20},{20,24},{24,28},{1,5},{5,9},{9,... | collective-permute-start | bytes 12296 | tf_op jit(solution)/shard_map/ppermute | solution.py:44
  101.9 3.1 %collective-permute-start.5 = (f32[1,8,128]{2,1,0:T(8,128)S(1)}, f32[1,8,128]{2,1,0:T(8,128)S(1)}, u32[]{:S(2)}, u32[]{:S(2)}) collective-permute-start(f32[1,8,128]{2,1,0:T(8,128)S(1)} %get-tuple-element.286), channel_id=1, source_target_pairs={{4,0},{8,4},{12,8},{16,12},{20,16},{24,20},{28,24},{5,1},{9,5},{13... | collective-permute-start | bytes 12296 | tf_op jit(solution)/shard_map/ppermute | solution.py:46
  105.5 0.6 copy-done.58
  106.2 1.0 fusion.23
  107.2 0.9 copy.161
  108.1 2.4 %collective-permute-start.6 = (f32[8,1,128]{2,1,0:T(1,128)S(1)}, f32[8,1,128]{2,1,0:T(1,128)S(1)}, u32[]{:S(2)}, u32[]{:S(2)}) collective-permute-start(f32[8,1,128]{2,1,0:T(1,128)S(1)} %get-tuple-element.274), channel_id=1, source_target_pairs={{0,1},{1,2},{2,3},{4,5},{5,6},{6,7},{8,9},{9,10},{10,11},{12,13},{... | collective-permute-start | bytes 12296 | tf_op jit(solution)/shard_map/ppermute | solution.py:44
  110.5 1.9 %collective-permute-start.7 = (f32[8,1,128]{2,1,0:T(1,128)S(1)}, f32[8,1,128]{2,1,0:T(1,128)S(1)}, u32[]{:S(2)}, u32[]{:S(2)}) collective-permute-start(f32[8,1,128]{2,1,0:T(1,128)S(1)} %get-tuple-element.273), channel_id=1, source_target_pairs={{1,0},{2,1},{3,2},{5,4},{6,5},{7,6},{9,8},{10,9},{11,10},{13,12},{... | collective-permute-start | bytes 12296 | tf_op jit(solution)/shard_map/ppermute | solution.py:46
  112.6 2.8 %collective-permute-done.7 = f32[8,1,128]{2,1,0:T(1,128)S(1)} collective-permute-done((f32[8,1,128]{2,1,0:T(1,128)S(1)}, f32[8,1,128]{2,1,0:T(1,128)S(1)}, u32[]{:S(2)}, u32[]{:S(2)}) %collective-permute-start.7) | collective-permute-done | bytes 4128 | tf_op jit(solution)/shard_map/ppermute | solution.py:46
  115.7 0.8 add_select_fusion
  (244 shorter events, 15.0 us)
Async XLA Ops:
  0.6 2.0 %copy-start = (f32[19,6,8,128]{3,2,1,0:T(8,128)S(1)}, f32[19,6,8,128]{3,2,1,0:T(8,128)}, u32[]{:S(2)}) copy-start(f32[19,6,8,128]{3,2,1,0:T(8,128)} %param.19) | copy-start | bytes 1400836
  1.8 8.0 %copy-start.3 = (f32[6,8,128]{2,1,0:T(8,128)}, f32[6,8,128]{2,1,0:T(8,128)S(1)}, u32[]{:S(2)}) copy-start(f32[6,8,128]{2,1,0:T(8,128)S(1)} %reduce_sum.45) | copy-start | bytes 73732
  2.6 59.5 %collective-permute-start = (f32[21,1,8,128]{3,2,1,0:T(8,128)S(1)}, f32[21,1,8,128]{3,2,1,0:T(8,128)S(1)}, u32[]{:S(2)}, u32[]{:S(2)}) collective-permute-start(f32[21,1,8,128]{3,2,1,0:T(8,128)S(1)} %get-tuple-element.139), channel_id=1, source_target_pairs={{0,4},{4,8},{8,12},{12,16},{16,20},{20,24},{24,28},{1,5},{5,9},{9,... | collective-permute-start | bytes 258056 | tf_op jit(solution)/shard_map/ppermute | solution.py:44
  5.7 56.4 %collective-permute-start.1 = (f32[21,1,8,128]{3,2,1,0:T(8,128)S(1)}, f32[21,1,8,128]{3,2,1,0:T(8,128)S(1)}, u32[]{:S(2)}, u32[]{:S(2)}) collective-permute-start(f32[21,1,8,128]{3,2,1,0:T(8,128)S(1)} %get-tuple-element.140), channel_id=1, source_target_pairs={{4,0},{8,4},{12,8},{16,12},{20,16},{24,20},{28,24},{5,1},{9,5},{13... | collective-permute-start | bytes 258056 | tf_op jit(solution)/shard_map/ppermute | solution.py:46
  62.3 7.2 %collective-permute-start.2 = (f32[21,8,1,128]{3,2,1,0:T(1,128)S(1)}, f32[21,8,1,128]{3,2,1,0:T(1,128)S(1)}, u32[]{:S(2)}, u32[]{:S(2)}) collective-permute-start(f32[21,8,1,128]{3,2,1,0:T(1,128)S(1)} %get-tuple-element.135), channel_id=1, source_target_pairs={{0,1},{1,2},{2,3},{4,5},{5,6},{6,7},{8,9},{9,10},{10,11},{12,13},{... | collective-permute-start | bytes 258056 | tf_op jit(solution)/shard_map/ppermute | solution.py:44
  67.6 5.8 %collective-permute-start.3 = (f32[21,8,1,128]{3,2,1,0:T(1,128)S(1)}, f32[21,8,1,128]{3,2,1,0:T(1,128)S(1)}, u32[]{:S(2)}, u32[]{:S(2)}) collective-permute-start(f32[21,8,1,128]{3,2,1,0:T(1,128)S(1)} %get-tuple-element.136), channel_id=1, source_target_pairs={{1,0},{2,1},{3,2},{5,4},{6,5},{7,6},{9,8},{10,9},{11,10},{13,12},{... | collective-permute-start | bytes 258056 | tf_op jit(solution)/shard_map/ppermute | solution.py:46
  91.3 3.0 %copy-start.14 = (pred[19,6,8,128]{3,2,1,0:T(8,128)(4,1)S(1)}, pred[19,6,8,128]{3,2,1,0:T(8,128)(4,1)}, u32[]{:S(2)}) copy-start(pred[19,6,8,128]{3,2,1,0:T(8,128)(4,1)} %copy-done.13) | copy-start | bytes 350212
  94.4 1.9 %copy-start.16 = (f32[6,8,1]{2,1,0:T(8,128)S(1)}, f32[6,8,1]{2,1,0:T(8,128)}, u32[]{:S(2)}) copy-start(f32[6,8,1]{2,1,0:T(8,128)} %get-tuple-element.242) | copy-start | bytes 580
  94.4 1.9 %copy-start.17 = (f32[6,8,1]{2,1,0:T(8,128)S(1)}, f32[6,8,1]{2,1,0:T(8,128)}, u32[]{:S(2)}) copy-start(f32[6,8,1]{2,1,0:T(8,128)} %get-tuple-element.243) | copy-start | bytes 580
  94.4 1.9 %copy-start.18 = (f32[6,8,1]{2,1,0:T(8,128)S(1)}, f32[6,8,1]{2,1,0:T(8,128)}, u32[]{:S(2)}) copy-start(f32[6,8,1]{2,1,0:T(8,128)} %get-tuple-element.244) | copy-start | bytes 580
  94.4 1.9 %copy-start.19 = (f32[6,8,1]{2,1,0:T(8,128)S(1)}, f32[6,8,1]{2,1,0:T(8,128)}, u32[]{:S(2)}) copy-start(f32[6,8,1]{2,1,0:T(8,128)} %get-tuple-element.245) | copy-start | bytes 580
  94.4 1.9 %copy-start.20 = (f32[6,8,1]{2,1,0:T(8,128)S(1)}, f32[6,8,1]{2,1,0:T(8,128)}, u32[]{:S(2)}) copy-start(f32[6,8,1]{2,1,0:T(8,128)} %get-tuple-element.246) | copy-start | bytes 580
  94.4 1.9 %copy-start.21 = (f32[6,8,1]{2,1,0:T(8,128)S(1)}, f32[6,8,1]{2,1,0:T(8,128)}, u32[]{:S(2)}) copy-start(f32[6,8,1]{2,1,0:T(8,128)} %get-tuple-element.247) | copy-start | bytes 580
  94.4 1.9 %copy-start.22 = (f32[6,8,1]{2,1,0:T(8,128)S(1)}, f32[6,8,1]{2,1,0:T(8,128)}, u32[]{:S(2)}) copy-start(f32[6,8,1]{2,1,0:T(8,128)} %get-tuple-element.248) | copy-start | bytes 580
  94.4 1.9 %copy-start.23 = (f32[6,8,1]{2,1,0:T(8,128)S(1)}, f32[6,8,1]{2,1,0:T(8,128)}, u32[]{:S(2)}) copy-start(f32[6,8,1]{2,1,0:T(8,128)} %get-tuple-element.249) | copy-start | bytes 580
  94.4 1.9 %copy-start.24 = (f32[6,8,127]{2,1,0:T(8,128)S(1)}, f32[6,8,127]{2,1,0:T(8,128)}, u32[]{:S(2)}) copy-start(f32[6,8,127]{2,1,0:T(8,128)} %get-tuple-element.250) | copy-start | bytes 73156
  94.5 1.9 %copy-start.25 = (f32[6,8,127]{2,1,0:T(8,128)S(1)}, f32[6,8,127]{2,1,0:T(8,128)}, u32[]{:S(2)}) copy-start(f32[6,8,127]{2,1,0:T(8,128)} %get-tuple-element.261) | copy-start | bytes 73156
  94.5 1.9 %copy-start.26 = (f32[6,8,127]{2,1,0:T(8,128)S(1)}, f32[6,8,127]{2,1,0:T(8,128)}, u32[]{:S(2)}) copy-start(f32[6,8,127]{2,1,0:T(8,128)} %get-tuple-element.262) | copy-start | bytes 73156
  94.5 1.9 %copy-start.27 = (f32[6,8,127]{2,1,0:T(8,128)S(1)}, f32[6,8,127]{2,1,0:T(8,128)}, u32[]{:S(2)}) copy-start(f32[6,8,127]{2,1,0:T(8,128)} %get-tuple-element.263) | copy-start | bytes 73156
  94.5 1.9 %copy-start.28 = (f32[6,8,127]{2,1,0:T(8,128)S(1)}, f32[6,8,127]{2,1,0:T(8,128)}, u32[]{:S(2)}) copy-start(f32[6,8,127]{2,1,0:T(8,128)} %get-tuple-element.264) | copy-start | bytes 73156
  94.5 1.9 %copy-start.29 = (f32[6,8,127]{2,1,0:T(8,128)S(1)}, f32[6,8,127]{2,1,0:T(8,128)}, u32[]{:S(2)}) copy-start(f32[6,8,127]{2,1,0:T(8,128)} %get-tuple-element.265) | copy-start | bytes 73156
  94.5 1.9 %copy-start.30 = (f32[6,8,127]{2,1,0:T(8,128)S(1)}, f32[6,8,127]{2,1,0:T(8,128)}, u32[]{:S(2)}) copy-start(f32[6,8,127]{2,1,0:T(8,128)} %get-tuple-element.266) | copy-start | bytes 73156
  94.5 1.9 %copy-start.31 = (f32[6,8,127]{2,1,0:T(8,128)S(1)}, f32[6,8,127]{2,1,0:T(8,128)}, u32[]{:S(2)}) copy-start(f32[6,8,127]{2,1,0:T(8,128)} %get-tuple-element.267) | copy-start | bytes 73156
  94.5 1.9 %copy-start.32 = (f32[6,8,127]{2,1,0:T(8,128)S(1)}, f32[6,8,127]{2,1,0:T(8,128)}, u32[]{:S(2)}) copy-start(f32[6,8,127]{2,1,0:T(8,128)} %get-tuple-element.268) | copy-start | bytes 73156
  94.5 1.9 %copy-start.33 = (f32[6,8,1]{2,1,0:T(8,128)S(1)}, f32[6,8,1]{2,1,0:T(8,128)}, u32[]{:S(2)}) copy-start(f32[6,8,1]{2,1,0:T(8,128)} %get-tuple-element.171) | copy-start | bytes 580
  94.5 1.9 %copy-start.34 = (f32[6,8,1]{2,1,0:T(8,128)S(1)}, f32[6,8,1]{2,1,0:T(8,128)}, u32[]{:S(2)}) copy-start(f32[6,8,1]{2,1,0:T(8,128)} %get-tuple-element.172) | copy-start | bytes 580
  94.6 1.9 %copy-start.35 = (f32[6,8,1]{2,1,0:T(8,128)S(1)}, f32[6,8,1]{2,1,0:T(8,128)}, u32[]{:S(2)}) copy-start(f32[6,8,1]{2,1,0:T(8,128)} %get-tuple-element.173) | copy-start | bytes 580
  94.6 1.9 %copy-start.36 = (f32[6,8,1]{2,1,0:T(8,128)S(1)}, f32[6,8,1]{2,1,0:T(8,128)}, u32[]{:S(2)}) copy-start(f32[6,8,1]{2,1,0:T(8,128)} %get-tuple-element.174) | copy-start | bytes 580
  94.6 1.9 %copy-start.37 = (f32[6,8,1]{2,1,0:T(8,128)S(1)}, f32[6,8,1]{2,1,0:T(8,128)}, u32[]{:S(2)}) copy-start(f32[6,8,1]{2,1,0:T(8,128)} %get-tuple-element.175) | copy-start | bytes 580
  94.6 1.9 %copy-start.38 = (f32[6,8,1]{2,1,0:T(8,128)S(1)}, f32[6,8,1]{2,1,0:T(8,128)}, u32[]{:S(2)}) copy-start(f32[6,8,1]{2,1,0:T(8,128)} %get-tuple-element.176) | copy-start | bytes 580
  94.6 1.9 %copy-start.39 = (f32[6,8,1]{2,1,0:T(8,128)S(1)}, f32[6,8,1]{2,1,0:T(8,128)}, u32[]{:S(2)}) copy-start(f32[6,8,1]{2,1,0:T(8,128)} %get-tuple-element.177) | copy-start | bytes 580
  94.6 1.9 %copy-start.40 = (f32[6,8,1]{2,1,0:T(8,128)S(1)}, f32[6,8,1]{2,1,0:T(8,128)}, u32[]{:S(2)}) copy-start(f32[6,8,1]{2,1,0:T(8,128)} %get-tuple-element.178) | copy-start | bytes 580
  94.6 1.9 %copy-start.41 = (f32[6,8,1]{2,1,0:T(8,128)S(1)}, f32[6,8,1]{2,1,0:T(8,128)}, u32[]{:S(2)}) copy-start(f32[6,8,1]{2,1,0:T(8,128)} %get-tuple-element.179) | copy-start | bytes 580
  94.6 1.9 %copy-start.42 = (f32[6,8,1]{2,1,0:T(8,128)S(1)}, f32[6,8,1]{2,1,0:T(8,128)}, u32[]{:S(2)}) copy-start(f32[6,8,1]{2,1,0:T(8,128)} %get-tuple-element.180) | copy-start | bytes 580
  94.6 1.9 %copy-start.43 = (f32[6,8,1]{2,1,0:T(8,128)S(1)}, f32[6,8,1]{2,1,0:T(8,128)}, u32[]{:S(2)}) copy-start(f32[6,8,1]{2,1,0:T(8,128)} %get-tuple-element.323) | copy-start | bytes 580
  94.6 1.9 %copy-start.44 = (f32[6,8,127]{2,1,0:T(8,128)S(1)}, f32[6,8,127]{2,1,0:T(8,128)}, u32[]{:S(2)}) copy-start(f32[6,8,127]{2,1,0:T(8,128)} %get-tuple-element.181) | copy-start | bytes 73156
  94.7 1.9 %copy-start.45 = (f32[6,8,127]{2,1,0:T(8,128)S(1)}, f32[6,8,127]{2,1,0:T(8,128)}, u32[]{:S(2)}) copy-start(f32[6,8,127]{2,1,0:T(8,128)} %get-tuple-element.182) | copy-start | bytes 73156
  94.7 1.9 %copy-start.46 = (f32[6,8,127]{2,1,0:T(8,128)S(1)}, f32[6,8,127]{2,1,0:T(8,128)}, u32[]{:S(2)}) copy-start(f32[6,8,127]{2,1,0:T(8,128)} %get-tuple-element.183) | copy-start | bytes 73156
  94.7 1.9 %copy-start.47 = (f32[6,8,127]{2,1,0:T(8,128)S(1)}, f32[6,8,127]{2,1,0:T(8,128)}, u32[]{:S(2)}) copy-start(f32[6,8,127]{2,1,0:T(8,128)} %get-tuple-element.184) | copy-start | bytes 73156
  94.7 1.9 %copy-start.48 = (f32[6,8,127]{2,1,0:T(8,128)S(1)}, f32[6,8,127]{2,1,0:T(8,128)}, u32[]{:S(2)}) copy-start(f32[6,8,127]{2,1,0:T(8,128)} %get-tuple-element.185) | copy-start | bytes 73156
  94.7 1.9 %copy-start.49 = (f32[6,8,127]{2,1,0:T(8,128)S(1)}, f32[6,8,127]{2,1,0:T(8,128)}, u32[]{:S(2)}) copy-start(f32[6,8,127]{2,1,0:T(8,128)} %get-tuple-element.186) | copy-start | bytes 73156
  94.7 1.9 %copy-start.50 = (f32[6,8,127]{2,1,0:T(8,128)S(1)}, f32[6,8,127]{2,1,0:T(8,128)}, u32[]{:S(2)}) copy-start(f32[6,8,127]{2,1,0:T(8,128)} %get-tuple-element.187) | copy-start | bytes 73156
  94.7 1.9 %copy-start.51 = (f32[6,8,127]{2,1,0:T(8,128)S(1)}, f32[6,8,127]{2,1,0:T(8,128)}, u32[]{:S(2)}) copy-start(f32[6,8,127]{2,1,0:T(8,128)} %get-tuple-element.188) | copy-start | bytes 73156
  98.8 6.2 %copy-start.70 = (f32[3,19,1,1]{1,0,3,2:T(4,128)S(1)}, f32[3,19,1,1]{1,0,3,2:T(4,128)}, u32[]{:S(2)}) copy-start(f32[3,19,1,1]{1,0,3,2:T(4,128)} %constant.143) | copy-start | bytes 688
  98.8 9.3 %collective-permute-start.4 = (f32[1,8,128]{2,1,0:T(8,128)S(1)}, f32[1,8,128]{2,1,0:T(8,128)S(1)}, u32[]{:S(2)}, u32[]{:S(2)}) collective-permute-start(f32[1,8,128]{2,1,0:T(8,128)S(1)} %get-tuple-element.285), channel_id=1, source_target_pairs={{0,4},{4,8},{8,12},{12,16},{16,20},{20,24},{24,28},{1,5},{5,9},{9,... | collective-permute-start | bytes 12296 | tf_op jit(solution)/shard_map/ppermute | solution.py:44
  101.9 6.2 %collective-permute-start.5 = (f32[1,8,128]{2,1,0:T(8,128)S(1)}, f32[1,8,128]{2,1,0:T(8,128)S(1)}, u32[]{:S(2)}, u32[]{:S(2)}) collective-permute-start(f32[1,8,128]{2,1,0:T(8,128)S(1)} %get-tuple-element.286), channel_id=1, source_target_pairs={{4,0},{8,4},{12,8},{16,12},{20,16},{24,20},{28,24},{5,1},{9,5},{13... | collective-permute-start | bytes 12296 | tf_op jit(solution)/shard_map/ppermute | solution.py:46
  108.1 4.5 %collective-permute-start.6 = (f32[8,1,128]{2,1,0:T(1,128)S(1)}, f32[8,1,128]{2,1,0:T(1,128)S(1)}, u32[]{:S(2)}, u32[]{:S(2)}) collective-permute-start(f32[8,1,128]{2,1,0:T(1,128)S(1)} %get-tuple-element.274), channel_id=1, source_target_pairs={{0,1},{1,2},{2,3},{4,5},{5,6},{6,7},{8,9},{9,10},{10,11},{12,13},{... | collective-permute-start | bytes 12296 | tf_op jit(solution)/shard_map/ppermute | solution.py:44
  110.5 4.9 %collective-permute-start.7 = (f32[8,1,128]{2,1,0:T(1,128)S(1)}, f32[8,1,128]{2,1,0:T(1,128)S(1)}, u32[]{:S(2)}, u32[]{:S(2)}) collective-permute-start(f32[8,1,128]{2,1,0:T(1,128)S(1)} %get-tuple-element.273), channel_id=1, source_target_pairs={{1,0},{2,1},{3,2},{5,4},{6,5},{7,6},{9,8},{10,9},{11,10},{13,12},{... | collective-permute-start | bytes 12296 | tf_op jit(solution)/shard_map/ppermute | solution.py:46
  (33 other events, 24.3 us)
